TPU v7x, 128 devices: a whole 4x4x4 slice. The times are simulated.
128 devices in a mesh: row: 16 (over z_hi, y, core), col: 8 (over x, z_lo).
Axes of the slice: x: 4, y: 4, z: 4 (z_hi: 2, z_lo: 2; z = z_hi * 2 + z_lo), core: 2. Of those that a mesh axis runs over, the one named last changes fastest.
Arguments:
- rotation: bfloat16 [8192, 8192], P('row', 'col'), may hold values from -0.0625 to 0.0625
- gradient: bfloat16 [8192, 8192], P('row', 'col'), may hold values from -0.0625 to 0.0625
Outputs:
- updated: float32 [8192, 2048], P('row', 'col')
- column_norms: float32 [2048], P('col')
All inputs are finite; a program needn't handle non-finite values.
Results may differ from a plain program's by a relative error of at most 0.01.
Values may be sent and summed in bfloat16 or wider, within the bound.
A program may use at most 128 MiB of HBM per device.

v0:
```python
import jax
import jax.numpy as jnp
from jax import lax
from jax.sharding import PartitionSpec as P

N = 8192
SLAB = 2048


def cut_along(array, dim, peers):
    before, after = (array.shape[:dim], array.shape[dim + 1 :])
    return jnp.moveaxis(array.reshape(*before, peers, -1, *after), dim, 0)


def summed_on_arrival(array, axis, dim):
    peers = lax.axis_size(axis)
    blocks = lax.all_to_all(cut_along(array, dim, peers), axis, 0, 0, tiled=True)
    return jnp.sum(blocks.astype(jnp.float32), axis=0)


def laid_out(blocks, dim):
    shape = list(blocks.shape[1:])
    shape[dim] *= blocks.shape[0]
    return jnp.moveaxis(blocks, 0, dim).reshape(shape)


def copy_for_each(array, axis):
    peers = lax.axis_size(axis)
    return lax.all_to_all(
        jnp.broadcast_to(array[None], (peers, *array.shape)), axis, 0, 0, tiled=True
    )


def gathered_copies(array, axis, dim):
    return laid_out(copy_for_each(array, axis), dim)


def over_copies(array, axis):
    everything = copy_for_each(array, axis)
    return jnp.sum(everything, axis=0)


def apply_generator(rotation, gradient, panel):
    left = jnp.einsum("ik,is->ks", rotation, panel, preferred_element_type=jnp.float32).astype(
        jnp.bfloat16
    )
    right = jnp.einsum("ik,is->ks", gradient, panel, preferred_element_type=jnp.float32).astype(
        jnp.bfloat16
    )
    left_sum, right_sum = (
        lax.psum(left, "row").astype(jnp.float32),
        lax.psum(right, "row").astype(jnp.float32),
    )
    left_full = left_sum.astype(jnp.bfloat16)
    right_full = right_sum.astype(jnp.bfloat16)
    term = jnp.dot(gradient, left_full, preferred_element_type=jnp.float32) - jnp.dot(
        rotation, right_full, preferred_element_type=jnp.float32
    )
    return summed_on_arrival(term.astype(jnp.bfloat16), "col", 1)


def on_device(rotation, gradient):
    stride = N // SLAB
    base = rotation[:, ::stride]
    rows_first = gathered_copies(base, "col", 1)
    base_wide = base.astype(jnp.float32)
    first = base_wide + 0.25 * apply_generator(rotation, gradient, rows_first)
    middle = (base_wide + first).astype(jnp.bfloat16)
    rows_again = gathered_copies(middle, "col", 1)
    updated = base_wide + 0.125 * apply_generator(rotation, gradient, rows_again)
    squares = over_copies(jnp.sum(updated * updated, axis=0), "row")
    return (updated, jnp.sqrt(squares))


def solution(mesh):
    placed = (P("row", "col"), P("row", "col"))
    return jax.shard_map(
        on_device,
        mesh=mesh,
        in_specs=placed,
        out_specs=(P("row", "col"), P("col")),
        check_vma=False,
    )
```

profile of v0, /device:TPU:1, one launch (start us, length us, event | category | flops | bytes accessed | tf_op | source)
XLA Modules:
  0.0 516.1 jit_solution(10673912607724911669)
XLA Ops:
  7.2 0.0 copy-start
  7.2 0.0 copy-start.1
  7.2 0.0 all-reduce.7.cloned.1.call-start
  7.2 11.1 %slice.3 = bf16[512,256]{1,0:T(8,128)(2,1)S(1)} slice(bf16[512,1024]{1,0:T(8,128)(2,1)} %param.2), slice={[0:512:1], [0:1024:4]} | slice | bytes 524288 | tf_op jit(solution)/shard_map/slice | solution.py:64
  18.3 0.1 copy.14
  18.5 0.2 broadcast_in_dim.6
  18.7 31.8 %all_to_all.26 = bf16[8,512,256]{1,2,0:T(8,128)(2,1)S(1)} all-to-all(bf16[8,512,256]{1,2,0:T(8,128)(2,1)S(1)} %broadcast_in_dim.6), channel_id=1, replica_groups=mesh['row'=16,'col'=8] {'col'}, dimensions={0} | all-to-all | bytes 4194304 | tf_op jit(solution)/shard_map/all_to_all | solution.py:29
  50.4 0.0 copy-done.1
  50.4 4.4 convolution_convert_fusion.1
  54.8 0.0 copy-done
  54.8 4.4 convolution_convert_fusion
  59.2 0.0 all-reduce.7.cloned.1.call-update
  59.2 0.2 all-reduce.5.cloned.1.call-start
  59.5 164.0 %all-reduce.7.cloned.1.call-done = (bf16[1024,2048]{1,0:T(8,128)(2,1)}, bf16[1024,2048]{1,0:T(8,128)(2,1)}) async-done(((bf16[1024,2048]{1,0:T(8,128)(2,1)}, bf16[1024,2048]{1,0:T(8,128)(2,1)}), (bf16[1024,2048]{1,0:T(8,128)(2,1)}, bf16[1024,2048]{1,0:T(8,128)(2,1)})) %all-reduce.7.cloned.1.call-update) | async-done | bytes 8388624 | tf_op jit(solution)/shard_map/psum | solution.py:51
  223.5 0.0 copy-start.2
  223.5 4.7 fusion.1
  228.3 0.0 copy-done.2
  228.3 2.4 subtract_convert_fusion.1
  230.7 28.1 %all_to_all.27 = bf16[8,512,256]{1,2,0:T(8,128)(2,1)S(1)} all-to-all(bf16[8,512,256]{1,2,0:T(8,128)(2,1)S(1)} %bitcast.38), channel_id=1, replica_groups=mesh['row'=16,'col'=8] {'col'}, dimensions={0} | all-to-all | bytes 4194304 | tf_op jit(solution)/shard_map/all_to_all | solution.py:17
  258.8 0.3 convert_reduce_fusion.1
  259.1 0.1 fusion
  259.2 0.2 broadcast_in_dim.7
  259.4 25.9 %all_to_all.28 = bf16[8,512,256]{1,2,0:T(8,128)(2,1)S(1)} all-to-all(bf16[8,512,256]{1,2,0:T(8,128)(2,1)S(1)} %broadcast_in_dim.7), channel_id=1, replica_groups=mesh['row'=16,'col'=8] {'col'}, dimensions={0} | all-to-all | bytes 4194304 | tf_op jit(solution)/shard_map/all_to_all | solution.py:29
  285.3 4.3 convert_bitcast_fusion
  289.6 4.3 convert_bitcast_fusion.1
  293.9 0.0 all-reduce.5.cloned.1.call-update
  293.9 163.7 %all-reduce.5.cloned.1.call-done = (bf16[1024,2048]{0,1:T(8,128)(2,1)}, bf16[1024,2048]{0,1:T(8,128)(2,1)}) async-done(((bf16[1024,2048]{0,1:T(8,128)(2,1)}, bf16[1024,2048]{0,1:T(8,128)(2,1)}), (bf16[1024,2048]{0,1:T(8,128)(2,1)}, bf16[1024,2048]{0,1:T(8,128)(2,1)})) %all-reduce.5.cloned.1.call-update) | async-done | bytes 8388624 | tf_op jit(solution)/shard_map/psum | solution.py:51
  457.6 0.0 copy-start.3
  457.6 4.7 fusion.2
  462.3 0.0 copy-done.3
  462.3 2.4 subtract_convert_fusion
  464.7 28.1 %all_to_all.29 = bf16[8,512,256]{1,2,0:T(8,128)(2,1)S(1)} all-to-all(bf16[8,512,256]{1,2,0:T(8,128)(2,1)S(1)} %bitcast.41), channel_id=1, replica_groups=mesh['row'=16,'col'=8] {'col'}, dimensions={0} | all-to-all | bytes 4194304 | tf_op jit(solution)/shard_map/all_to_all | solution.py:17
  492.8 0.3 convert_reduce_fusion
  493.1 0.2 multiply_reduce_fusion
  493.3 0.6 broadcast_in_dim.8
  493.9 7.4 %all-to-all-start.4 = ((f32[16,1,256]{2,1,0:T(1,128)}), f32[16,1,256]{2,1,0:T(1,128)S(1)}, u32[]{:S(2)}, u32[]{:S(2)}) async-start(f32[16,1,256]{2,1,0:T(1,128)} %broadcast_in_dim.8), calls=%async_computation.4 | async-start | bytes 32768 | tf_op jit(solution)/shard_map/all_to_all | solution.py:29
  501.3 1.0 copy.12
  502.3 6.3 %all-to-all-done.4 = f32[16,1,256]{2,1,0:T(1,128)S(1)} async-done(((f32[16,1,256]{2,1,0:T(1,128)}), f32[16,1,256]{2,1,0:T(1,128)S(1)}, u32[]{:S(2)}, u32[]{:S(2)}) %all-to-all-start.4) | async-done | bytes 16416 | tf_op jit(solution)/shard_map/all_to_all | solution.py:29
  508.6 0.6 sqrt.3
  (1 shorter events, 0.0 us)
Async XLA Ops:
  7.2 47.7 %copy-start = (bf16[512,1024]{1,0:T(8,128)(2,1)S(1)}, bf16[512,1024]{1,0:T(8,128)(2,1)}, u32[]{:S(2)}) copy-start(bf16[512,1024]{1,0:T(8,128)(2,1)} %param.3) | copy-start | bytes 3145732
  7.2 43.3 %copy-start.1 = (bf16[512,1024]{1,0:T(8,128)(2,1)S(1)}, bf16[512,1024]{1,0:T(8,128)(2,1)}, u32[]{:S(2)}) copy-start(bf16[512,1024]{1,0:T(8,128)(2,1)} %param.2) | copy-start | bytes 3145732
  7.2 216.3 %all-reduce.7.cloned.1.call-start = ((), (), s32[]{:S(2)}) async-start(), calls=%async_computation.6 | async-start | bytes 16777216 | tf_op jit(solution)/shard_map/psum | solution.py:51
  59.2 398.4 %all-reduce.5.cloned.1.call-start = ((), (), s32[]{:S(2)}) async-start(), calls=%async_computation.5 | async-start | bytes 16777216 | tf_op jit(solution)/shard_map/psum | solution.py:51
  223.5 4.7 copy-start.2
  457.6 4.7 copy-start.3
  493.9 14.7 %all-to-all-start.4 = ((f32[16,1,256]{2,1,0:T(1,128)}), f32[16,1,256]{2,1,0:T(1,128)S(1)}, u32[]{:S(2)}, u32[]{:S(2)}) async-start(f32[16,1,256]{2,1,0:T(1,128)} %broadcast_in_dim.8), calls=%async_computation.4 | async-start | bytes 32768 | tf_op jit(solution)/shard_map/all_to_all | solution.py:29
Sparse Core Ops, SparseCore 0:
  59.4 164.1 all-reduce.6
  294.0 163.5 all-reduce.4
where the time goes:
time: 516 us
  waiting for transfers between devices  334 us (65%)
  blocking collectives  114 us (22%)
  matrix products  31.6 us (6%)
  between operations  14.2 us (3%)
  local copies, waits for them, and re-layouts  13.8 us (3%)
  starting transfers between devices  7.63 us (1%)
    psum x2, waiting for transfers between devices, apply_generator(): lax.psum(left, 'row').astype(jnp.float32)  328 us
    all_to_all x2, blocking collectives, copy_for_each(): lax.all_to_all(jnp.broadcast_to(array[None], (peers, *array.shape)), axis...  57.7 us
    all_to_all x2, blocking collectives, summed_on_arrival(): lax.all_to_all(cut_along(array, dim, peers), axis, 0, 0, tiled=True)  56.2 us
    slice x1, local copies, waits for them, and re-layouts, on_device(): base = rotation[:, ::stride]  11.1 us
  transfers between devices with their start and end apart: 3, of which 3 were waited for; matrix products, arithmetic and copies ran while one was open for 0% of the time, Pallas kernels for 0%

commit v1 on v0

v1 whole, which is shorter than its diff:
```python
import jax
import jax.numpy as jnp
from jax import lax
from jax.experimental import pallas as pl
from jax.experimental.pallas import tpu as pltpu
from jax.sharding import PartitionSpec as P

MESH = pl.DeviceIdType.MESH
F32 = jnp.float32
BF16 = jnp.bfloat16
NS = 4
CH = 32
BLK = 1024
HALF = 512
TILE = 512
ITEMS = 2 * NS


def step_kernel(
    rot_hbm, grad_hbm, out_ref, norm_ref,
    rot, grad, base, panel, part, full, mine, ring_a, ring_b, swapped,
    term, term_in, kept, tail, tail_in, upd, turned, turned_in, sq, sq_y, sq_sum, sq_in,
    load_sem, pair_s, pair_r, v0_s, v0_r, v1_s, v1_r, a_s, a_r, b_s, b_r, z_s, z_r,
    c_s, c_r, e_s, e_r, t_s, t_r, w_s, w_r, u_s, u_r, n_s, n_r, m_s, m_r,
):
    row = lax.axis_index("row")
    col = lax.axis_index("col")
    core, y, zh = row % 2, (row // 2) % 4, row // 8
    x, zl = col // 2, col % 2
    up, across, down = (y + 1) % 4, (y + 2) % 4, (y + 3) % 4

    def at_row(zh_, y_, core_):
        return {"row": zh_ * 8 + y_ * 2 + core_, "col": col}

    def at_col(x_, zl_):
        return {"row": row, "col": x_ * 2 + zl_}

    pair = at_row(zh, y, 1 - core)
    y_dev = (at_row(zh, up, core), at_row(zh, down, core))
    y_q = (up, down)
    y_all = tuple(at_row(zh, (y + k) % 4, core) for k in (1, 2, 3))
    z_dev = at_row(1 - zh, y, core)
    zc_dev = at_row(1 - zh, y, 1 - core)
    x_all = tuple(at_col((x + k) % 4, zl) for k in (1, 2, 3))
    zl_dev = at_col(x, 1 - zl)

    def send(src, dst, s, r, dev):
        return pltpu.make_async_remote_copy(
            src_ref=src, dst_ref=dst, send_sem=s, recv_sem=r, device_id=dev, device_id_type=MESH
        )

    own_rows = pl.ds(pl.multiple_of(core * HALF, HALF), HALF)
    other_rows = pl.ds(pl.multiple_of((1 - core) * HALF, HALF), HALF)
    loads = [
        pltpu.make_async_copy(rot_hbm, rot.at[own_rows], load_sem.at[0]),
        pltpu.make_async_copy(grad_hbm, grad.at[own_rows], load_sem.at[1]),
    ]
    for c in loads:
        c.start()

    barrier = pltpu.get_barrier_semaphore()
    peers = (pair, *y_all, z_dev, zc_dev, *x_all, zl_dev)
    for dev in peers:
        pl.semaphore_signal(barrier, inc=1, device_id=dev, device_id_type=MESH)
    pl.semaphore_wait(barrier, len(peers))

    pairs = [
        send(m.at[own_rows], m.at[own_rows], pair_s.at[k], pair_r.at[k], pair)
        for k, m in enumerate((rot, grad))
    ]
    for c, p in zip(loads, pairs):
        c.wait()
        p.start()
    pairs[0].wait_recv()

    pick = lax.broadcasted_iota(jnp.int32, (128, HALF), 1) == 4 * lax.broadcasted_iota(
        jnp.int32, (128, HALF), 0
    )
    base[...] = (
        lax.dot_general(
            pick.astype(F32).astype(BF16),
            rot[:, pl.ds(pl.multiple_of(core * HALF, HALF), HALF)],
            (((1,), (1,)), ((), ())),
            preferred_element_type=F32,
        )
        .astype(BF16)
        .reshape(NS, CH, BLK)
    )

    def v0(i):
        k = i % NS
        return send(panel.at[k, x, zl], panel.at[k, x, zl], v0_s.at[k], v0_r.at[k], zl_dev)

    def v1(i, d):
        k = i % NS
        return send(panel.at[k, x], panel.at[k, x], v1_s.at[k, d], v1_r.at[k, d], x_all[d])

    def ra(i, h, d):
        k = i % NS
        return send(
            part.at[k, h, across, d], ring_a.at[k, h, d], a_s.at[k, h, d], a_r.at[k, h, d], y_dev[d]
        )

    def rb(i, h, d):
        k = i % NS
        return send(
            part.at[k, h, y_q[d]], ring_b.at[k, h, d], b_s.at[k, h, d], b_r.at[k, h, d], y_dev[d]
        )

    def zx(i, h):
        k = i % NS
        return send(mine.at[k, h], swapped.at[k, h], z_s.at[k, h], z_r.at[k, h], z_dev)

    def ga(i, h, d):
        k = i % NS
        return send(
            full.at[k, h, y], full.at[k, h, y], c_s.at[k, h, d], c_r.at[k, h, d], y_dev[d]
        )

    def gb(i, h, d):
        k = i % NS
        q = y_q[1 - d]
        return send(
            full.at[k, h, q, d], full.at[k, h, q, d], e_s.at[k, h, d], e_r.at[k, h, d], y_dev[d]
        )

    def tx(i, d):
        k = i % NS
        return send(
            term.at[k, (x + d + 1) % 4], term_in.at[k, d], t_s.at[k, d], t_r.at[k, d], x_all[d]
        )

    def wz(i):
        k = i % NS
        return send(tail.at[k], tail_in.at[k], w_s.at[k], w_r.at[k], zl_dev)

    for j in range(NS):
        panel[j, x, zl] = base[j]
    for j in range(NS):
        v0(j).start()
    for j in range(NS):
        v0(j).wait_recv()
        for d in range(3):
            v1(j, d).start()
    pairs[1].wait_recv()

    def project(i, h):
        k = i % NS
        held = (rot, grad)[h]
        lhs = panel[k].reshape(8 * CH, BLK)

        @pl.loop(0, BLK // TILE)
        def _(n):
            cols = pl.ds(pl.multiple_of(n * TILE, TILE), TILE)
            z = jnp.dot(lhs, held[:, cols], preferred_element_type=F32)
            part[k, h, :, :, :, cols] = z.astype(BF16).reshape(4, 2, CH, TILE)

    def apply(i):
        k = i % NS

        @pl.loop(0, BLK // TILE)
        def _(n):
            rows = pl.ds(pl.multiple_of(n * TILE, TILE), TILE)
            nt = (((1,), (1,)), ((), ()))
            t = lax.dot_general(
                full[k, 0].reshape(8 * CH, BLK), grad[rows, :], nt, preferred_element_type=F32
            ) - lax.dot_general(
                full[k, 1].reshape(8 * CH, BLK), rot[rows, :], nt, preferred_element_type=F32
            )
            term[k, :, :, :, rows] = t.astype(BF16).reshape(4, 2, CH, TILE)

    def run(i, _):
        with_b = (i >= 1) & (i <= ITEMS)
        with_c = (i >= 2) & (i <= ITEMS + 1)
        with_d = (i >= 3) & (i <= ITEMS + 2)
        with_v = (i >= NS) & (i < ITEMS)

        @pl.when(with_b)
        def _():
            it = i - 1
            for d in range(3):
                v1(it, d).wait_recv()
            for h in range(2):
                project(it, h)
                for d in range(2):
                    ra(it, h, d).start()
            v0(it).wait_send()

        @pl.when(with_d)
        def _():
            it = i - 3
            for h in range(2):
                for d in range(2):
                    ga(it, h, d).wait_recv()
                for d in range(2):
                    gb(it, h, d).start()
            for h in range(2):
                zx(it, h).wait_send()

        @pl.when(i >= NS)
        def _():
            it = i - NS
            k = it % NS
            wz(it).wait_recv()
            applied = kept[k] + tail_in[k].astype(F32)
            b = base[k].astype(F32)

            @pl.when(i < ITEMS)
            def _():
                first = b + 0.25 * applied
                panel[k, x, zl] = (b + first).astype(BF16)
                v0(i).start()

            @pl.when(i >= ITEMS)
            def _():
                upd[k] = b + 0.125 * applied

            for d in range(3):
                tx(it, d).wait_send()
            wz(it).wait_send()

        @pl.when(with_b)
        def _():
            it = i - 1
            k = it % NS
            for h in range(2):
                for d in range(2):
                    ra(it, h, d).wait_recv()
                    total = part[k, h, y_q[d], d].astype(F32) + ring_a[k, h, d].astype(F32)
                    part[k, h, y_q[d], d] = total.astype(BF16)
                    rb(it, h, d).start()
            for d in range(3):
                v1(it, d).wait_send()

        @pl.when(with_v)
        def _():
            v0(i).wait_recv()
            for d in range(3):
                v1(i, d).start()

        @pl.when(with_d)
        def _():
            it = i - 3
            for h in range(2):
                for d in range(2):
                    gb(it, h, d).wait_recv()
            apply(it)
            for d in range(3):
                tx(it, d).start()
            for h in range(2):
                for d in range(2):
                    ga(it, h, d).wait_send()

        @pl.when(with_c)
        def _():
            it = i - 2
            k = it % NS
            for h in range(2):
                zx(it, h).wait_recv()
                z = mine[k, h].astype(F32) + swapped[k, h].astype(F32)
                full[k, h, y] = z.astype(BF16)
                for d in range(2):
                    ga(it, h, d).start()
            for h in range(2):
                for d in range(2):
                    rb(it, h, d).wait_send()

        @pl.when(with_b)
        def _():
            it = i - 1
            k = it % NS
            for h in range(2):
                for d in range(2):
                    rb(it, h, d).wait_recv()
                s = part[k, h, y].astype(F32) + (
                    ring_b[k, h, 0].astype(F32) + ring_b[k, h, 1].astype(F32)
                )
                mine[k, h] = s.astype(BF16)
                zx(it, h).start()
            for h in range(2):
                for d in range(2):
                    ra(it, h, d).wait_send()

        @pl.when(with_d)
        def _():
            it = i - 3
            k = it % NS
            for d in range(3):
                tx(it, d).wait_recv()

            def summed(z):
                return (term[k, x, z].astype(F32) + term_in[k, 0, z].astype(F32)) + (
                    term_in[k, 1, z].astype(F32) + term_in[k, 2, z].astype(F32)
                )

            tail[k] = summed(1 - zl).astype(BF16)
            wz(it).start()
            kept[k] = summed(zl)
            for h in range(2):
                for d in range(2):
                    gb(it, h, d).wait_send()

        return 0

    lax.fori_loop(1, ITEMS + NS, run, 0)

    total = jnp.zeros((1, 128), F32)
    for r in range(BLK // 128):
        block = upd[:, :, r * 128 : (r + 1) * 128].reshape(128, 128).T
        turned[r * 128 : (r + 1) * 128, :] = block
        total = total + jnp.sum(block * block, axis=0, keepdims=True)
    sq[...] = jnp.broadcast_to(total, (8, 128))
    swap = send(turned.at[other_rows], turned_in, u_s.at[0], u_r.at[0], pair)
    swap.start()
    ys = [send(sq, sq_y.at[k], n_s.at[k], n_r.at[k], y_all[k]) for k in range(3)]
    for c in ys:
        c.start()
    out_ref[:, pl.ds(pl.multiple_of(core * 128, 128), 128)] = turned[own_rows, :]
    for c in ys:
        c.wait_recv()
    sq_sum[...] = (sq[...] + sq_y[0]) + (sq_y[1] + sq_y[2])
    ms = [
        send(sq_sum, sq_in.at[k], m_s.at[k], m_r.at[k], dev)
        for k, dev in enumerate((z_dev, pair, zc_dev))
    ]
    for c in ms:
        c.start()
    swap.wait_recv()
    out_ref[:, pl.ds(pl.multiple_of((1 - core) * 128, 128), 128)] = turned_in[...]
    for c in ms:
        c.wait_recv()
    own_norm = jnp.sqrt(sq_sum[0:1, :] + sq_in[0, 0:1, :])
    other_norm = jnp.sqrt(sq_in[1, 0:1, :] + sq_in[2, 0:1, :])
    norm_ref[0:1, :] = jnp.where(core == 0, own_norm, other_norm)
    norm_ref[1:2, :] = jnp.where(core == 0, other_norm, own_norm)
    for c in (*pairs, swap, *ys, *ms):
        c.wait_send()


def on_device(rotation, gradient):
    dma = pltpu.SemaphoreType.DMA

    def both(shape):
        return [dma(shape), dma(shape)]

    quarters = (4, 2, CH, BLK)
    updated, norms = pl.pallas_call(
        step_kernel,
        name="cayley_step",
        out_shape=(
            jax.ShapeDtypeStruct((HALF, 256), F32),
            jax.ShapeDtypeStruct((2, 128), F32),
        ),
        in_specs=[pl.BlockSpec(memory_space=pl.ANY)] * 2,
        out_specs=(
            pl.BlockSpec(memory_space=pltpu.VMEM),
            pl.BlockSpec(memory_space=pltpu.VMEM),
        ),
        scratch_shapes=[
            pltpu.VMEM((BLK, BLK), BF16),
            pltpu.VMEM((BLK, BLK), BF16),
            pltpu.VMEM((NS, CH, BLK), BF16),
            pltpu.VMEM((NS, *quarters), BF16),
            pltpu.VMEM((NS, 2, *quarters), BF16),
            pltpu.VMEM((NS, 2, *quarters), BF16),
            pltpu.VMEM((NS, 2, 2, CH, BLK), BF16),
            pltpu.VMEM((NS, 2, 2, CH, BLK), BF16),
            pltpu.VMEM((NS, 2, 2, 2, CH, BLK), BF16),
            pltpu.VMEM((NS, 2, 2, CH, BLK), BF16),
            pltpu.VMEM((NS, *quarters), BF16),
            pltpu.VMEM((NS, 3, 2, CH, BLK), BF16),
            pltpu.VMEM((NS, CH, BLK), F32),
            pltpu.VMEM((NS, CH, BLK), BF16),
            pltpu.VMEM((NS, CH, BLK), BF16),
            pltpu.VMEM((NS, CH, BLK), F32),
            pltpu.VMEM((BLK, 128), F32),
            pltpu.VMEM((HALF, 128), F32),
            pltpu.VMEM((8, 128), F32),
            pltpu.VMEM((3, 8, 128), F32),
            pltpu.VMEM((8, 128), F32),
            pltpu.VMEM((3, 8, 128), F32),
            dma((2,)),
            *both((2,)),
            *both((NS,)),
            *both((NS, 3)),
            *both((NS, 2, 2)),
            *both((NS, 2, 2)),
            *both((NS, 2)),
            *both((NS, 2, 2)),
            *both((NS, 2, 2)),
            *both((NS, 3)),
            *both((NS,)),
            *both((1,)),
            *both((3,)),
            *both((3,)),
        ],
        compiler_params=pltpu.CompilerParams(
            collective_id=1, has_side_effects=True, vmem_limit_bytes=62 * 1024 * 1024
        ),
        cost_estimate=pl.CostEstimate(
            flops=20_000_000_000, bytes_accessed=3_000_000, transcendentals=0
        ),
    )(rotation, gradient)
    return updated, norms.reshape(256)


def solution(mesh):
    placed = (P("row", "col"), P("row", "col"))
    return jax.shard_map(
        on_device,
        mesh=mesh,
        in_specs=placed,
        out_specs=(P("row", "col"), P("col")),
        check_vma=False,
    )
```

time: 516 us -> 201 us (0.39)
  waiting for transfers between devices: 334 us -> 0 us
  Pallas kernels: 0 us -> 198 us
  blocking collectives: 114 us -> 0 us
  matrix products: 31.6 us -> 0 us
  between operations: 14.2 us -> 0.65 us
  local copies, waits for them, and re-layouts: 13.8 us -> 2.44 us
  starting transfers between devices: 7.63 us -> 0 us
    psum x2 -> x0, waiting for transfers between devices: 328 us -> none  [apply_generator(): lax.psum(left, 'row').astype(jnp.float32)]
    pallas_call x0 -> x1, Pallas kernels: none -> 198 us  [on_device(): pl.pallas_call(step_kernel, name='cayley_step', out_shape=(jax.ShapeDtype...]
    all_to_all x4 -> x0, blocking collectives: 114 us -> none  [the longest x2 57.7 us: copy_for_each(): lax.all_to_all(jnp.broadcast_to(array[None], (peers, *array.shape)), axis...]
    dot_general x8 -> x0, matrix products: 31.6 us -> none  [the longest x2 9.45 us: apply_generator(): jnp.dot(gradient, left_full, preferred_element_type=jnp.float32)]
    slice x1 -> x0, local copies, waits for them, and re-layouts: 11.1 us -> none  [on_device(): base = rotation[:, ::stride]]
    all_to_all x1 -> x0, starting transfers between devices: 7.37 us -> none  [copy_for_each(): lax.all_to_all(jnp.broadcast_to(array[None], (peers, *array.shape)), axis...]
    all_to_all x1 -> x0, waiting for transfers between devices: 6.3 us -> none  [copy_for_each(): lax.all_to_all(jnp.broadcast_to(array[None], (peers, *array.shape)), axis...]
  transfers between devices with their start and end apart: 3 -> 0, of which waited for: 3 -> 0; matrix products, arithmetic and copies ran while one was open for 0% -> 0% of each run, Pallas kernels for 0% -> 0%
where the time goes in v1:
time: 201 us
  Pallas kernels  198 us (99%)
  local copies, waits for them, and re-layouts  2.44 us (1%)
    pallas_call x1, Pallas kernels, on_device(): pl.pallas_call(step_kernel, name='cayley_step', out_shape=(jax.ShapeDtype...  198 us

profile of v1, /device:TPU:1, one launch (start us, length us, event | category | flops | bytes accessed | tf_op | source)
XLA Modules:
  0.0 201.0 jit_solution(5943597975850253606)
XLA Ops:
  0.6 197.9 %cayley_step.1 = (f32[512,256]{1,0:T(8,128)}, f32[2,128]{1,0:T(2,128)}) custom-call(bf16[512,1024]{1,0:T(8,128)(2,1)} %rot_hbm.1, bf16[512,1024]{1,0:T(8,128)(2,1)} %grad_hbm.1), custom_call_target="tpu_custom_call" | custom-call | flops 20000000000 | bytes 3000000 | tf_op jit(solution)/shard_map/cayley_step/pallas_call | solution.py:347
  198.6 0.0 copy-start
  198.6 1.9 copy.6
  200.5 0.0 copy-done
  200.5 0.6 copy.7
Async XLA Ops:
  198.6 1.9 copy-start

commit v2 on v1

--- a/solution.py
+++ b/solution.py
@@ -8,8 +8,8 @@
 MESH = pl.DeviceIdType.MESH
 F32 = jnp.float32
 BF16 = jnp.bfloat16
-NS = 4
-CH = 32
+NS = 8
+CH = 16
 BLK = 1024
 HALF = 512
 TILE = 512
@@ -18,7 +18,7 @@
 
 def step_kernel(
     rot_hbm, grad_hbm, out_ref, norm_ref,
-    rot, grad, base, panel, part, full, mine, ring_a, ring_b, swapped,
+    rot, grad, base, base_out, panel, part, full, mine, ring_a, ring_b, swapped,
     term, term_in, kept, tail, tail_in, upd, turned, turned_in, sq, sq_y, sq_sum, sq_in,
     load_sem, pair_s, pair_r, v0_s, v0_r, v1_s, v1_r, a_s, a_r, b_s, b_r, z_s, z_r,
     c_s, c_r, e_s, e_r, t_s, t_r, w_s, w_r, u_s, u_r, n_s, n_r, m_s, m_r,
@@ -62,30 +62,36 @@
     peers = (pair, *y_all, z_dev, zc_dev, *x_all, zl_dev)
     for dev in peers:
         pl.semaphore_signal(barrier, inc=1, device_id=dev, device_id_type=MESH)
-    pl.semaphore_wait(barrier, len(peers))
-
-    pairs = [
-        send(m.at[own_rows], m.at[own_rows], pair_s.at[k], pair_r.at[k], pair)
-        for k, m in enumerate((rot, grad))
-    ]
-    for c, p in zip(loads, pairs):
-        c.wait()
-        p.start()
-    pairs[0].wait_recv()
 
     pick = lax.broadcasted_iota(jnp.int32, (128, HALF), 1) == 4 * lax.broadcasted_iota(
         jnp.int32, (128, HALF), 0
     )
-    base[...] = (
-        lax.dot_general(
-            pick.astype(F32).astype(BF16),
-            rot[:, pl.ds(pl.multiple_of(core * HALF, HALF), HALF)],
-            (((1,), (1,)), ((), ())),
-            preferred_element_type=F32,
-        )
-        .astype(BF16)
-        .reshape(NS, CH, BLK)
-    )
+    pick = pick.astype(F32).astype(BF16)
+
+    def picked(side):
+        cols = pl.ds(pl.multiple_of(side * HALF, HALF), HALF)
+        return (
+            lax.dot_general(
+                pick, rot[own_rows, cols], (((1,), (1,)), ((), ())), preferred_element_type=F32
+            )
+            .astype(BF16)
+            .reshape(NS, CH, HALF)
+        )
+
+    loads[0].wait()
+    base_out[...] = picked(1 - core)
+    base[:, :, own_rows] = picked(core)
+    loads[1].wait()
+
+    pl.semaphore_wait(barrier, len(peers))
+    pairs = [
+        send(base_out, base.at[:, :, own_rows], pair_s.at[0], pair_r.at[0], pair),
+        send(rot.at[own_rows], rot.at[own_rows], pair_s.at[1], pair_r.at[1], pair),
+        send(grad.at[own_rows], grad.at[own_rows], pair_s.at[2], pair_r.at[2], pair),
+    ]
+    for c in pairs:
+        c.start()
+    pairs[0].wait_recv()
 
     def v0(i):
         k = i % NS
@@ -143,6 +149,7 @@
         for d in range(3):
             v1(j, d).start()
     pairs[1].wait_recv()
+    pairs[2].wait_recv()
 
     def project(i, h):
         k = i % NS
@@ -169,26 +176,15 @@
             )
             term[k, :, :, :, rows] = t.astype(BF16).reshape(4, 2, CH, TILE)
 
+    every = [(h, d) for h in range(2) for d in range(2)]
+
     def run(i, _):
-        with_b = (i >= 1) & (i <= ITEMS)
-        with_c = (i >= 2) & (i <= ITEMS + 1)
-        with_d = (i >= 3) & (i <= ITEMS + 2)
-        with_v = (i >= NS) & (i < ITEMS)
-
-        @pl.when(with_b)
-        def _():
-            it = i - 1
-            for d in range(3):
-                v1(it, d).wait_recv()
-            for h in range(2):
-                project(it, h)
-                for d in range(2):
-                    ra(it, h, d).start()
-            v0(it).wait_send()
-
-        @pl.when(with_d)
-        def _():
-            it = i - 3
+        def stage(late):
+            return pl.when((i >= late) & (i < ITEMS + late))
+
+        @stage(5)
+        def _():
+            it = i - 5
             for h in range(2):
                 for d in range(2):
                     ga(it, h, d).wait_recv()
@@ -197,63 +193,9 @@
             for h in range(2):
                 zx(it, h).wait_send()
 
-        @pl.when(i >= NS)
-        def _():
-            it = i - NS
-            k = it % NS
-            wz(it).wait_recv()
-            applied = kept[k] + tail_in[k].astype(F32)
-            b = base[k].astype(F32)
-
-            @pl.when(i < ITEMS)
-            def _():
-                first = b + 0.25 * applied
-                panel[k, x, zl] = (b + first).astype(BF16)
-                v0(i).start()
-
-            @pl.when(i >= ITEMS)
-            def _():
-                upd[k] = b + 0.125 * applied
-
-            for d in range(3):
-                tx(it, d).wait_send()
-            wz(it).wait_send()
-
-        @pl.when(with_b)
-        def _():
-            it = i - 1
-            k = it % NS
-            for h in range(2):
-                for d in range(2):
-                    ra(it, h, d).wait_recv()
-                    total = part[k, h, y_q[d], d].astype(F32) + ring_a[k, h, d].astype(F32)
-                    part[k, h, y_q[d], d] = total.astype(BF16)
-                    rb(it, h, d).start()
-            for d in range(3):
-                v1(it, d).wait_send()
-
-        @pl.when(with_v)
-        def _():
-            v0(i).wait_recv()
-            for d in range(3):
-                v1(i, d).start()
-
-        @pl.when(with_d)
-        def _():
-            it = i - 3
-            for h in range(2):
-                for d in range(2):
-                    gb(it, h, d).wait_recv()
-            apply(it)
-            for d in range(3):
-                tx(it, d).start()
-            for h in range(2):
-                for d in range(2):
-                    ga(it, h, d).wait_send()
-
-        @pl.when(with_c)
-        def _():
-            it = i - 2
+        @stage(4)
+        def _():
+            it = i - 4
             k = it % NS
             for h in range(2):
                 zx(it, h).wait_recv()
@@ -261,13 +203,12 @@
                 full[k, h, y] = z.astype(BF16)
                 for d in range(2):
                     ga(it, h, d).start()
-            for h in range(2):
-                for d in range(2):
-                    rb(it, h, d).wait_send()
-
-        @pl.when(with_b)
-        def _():
-            it = i - 1
+            for h, d in every:
+                rb(it, h, d).wait_send()
+
+        @stage(3)
+        def _():
+            it = i - 3
             k = it % NS
             for h in range(2):
                 for d in range(2):
@@ -277,13 +218,63 @@
                 )
                 mine[k, h] = s.astype(BF16)
                 zx(it, h).start()
-            for h in range(2):
-                for d in range(2):
-                    ra(it, h, d).wait_send()
-
-        @pl.when(with_d)
-        def _():
-            it = i - 3
+            for h, d in every:
+                ra(it, h, d).wait_send()
+
+        @stage(8)
+        def _():
+            it = i - 8
+            k = it % NS
+            wz(it).wait_recv()
+            applied = kept[k] + tail_in[k].astype(F32)
+            b = base[k].astype(F32)
+
+            @pl.when(i < ITEMS)
+            def _():
+                first = b + 0.25 * applied
+                panel[k, x, zl] = (b + first).astype(BF16)
+                v0(i).start()
+
+            @pl.when(i >= ITEMS)
+            def _():
+                upd[k] = b + 0.125 * applied
+
+            for d in range(3):
+                tx(it, d).wait_send()
+            wz(it).wait_send()
+
+        @stage(2)
+        def _():
+            it = i - 2
+            k = it % NS
+            for h, d in every:
+                ra(it, h, d).wait_recv()
+                total = part[k, h, y_q[d], d].astype(F32) + ring_a[k, h, d].astype(F32)
+                part[k, h, y_q[d], d] = total.astype(BF16)
+                rb(it, h, d).start()
+            for d in range(3):
+                v1(it, d).wait_send()
+
+        @stage(6)
+        def _():
+            it = i - 6
+            for h, d in every:
+                gb(it, h, d).wait_recv()
+            apply(it)
+            for d in range(3):
+                tx(it, d).start()
+            for h, d in every:
+                ga(it, h, d).wait_send()
+
+        @pl.when((i >= NS) & (i < ITEMS))
+        def _():
+            v0(i).wait_recv()
+            for d in range(3):
+                v1(i, d).start()
+
+        @stage(7)
+        def _():
+            it = i - 7
             k = it % NS
             for d in range(3):
                 tx(it, d).wait_recv()
@@ -296,13 +287,23 @@
             tail[k] = summed(1 - zl).astype(BF16)
             wz(it).start()
             kept[k] = summed(zl)
+            for h, d in every:
+                gb(it, h, d).wait_send()
+
+        @stage(1)
+        def _():
+            it = i - 1
+            for d in range(3):
+                v1(it, d).wait_recv()
             for h in range(2):
+                project(it, h)
                 for d in range(2):
-                    gb(it, h, d).wait_send()
+                    ra(it, h, d).start()
+            v0(it).wait_send()
 
         return 0
 
-    lax.fori_loop(1, ITEMS + NS, run, 0)
+    lax.fori_loop(1, ITEMS + 8, run, 0)
 
     total = jnp.zeros((1, 128), F32)
     for r in range(BLK // 128):
@@ -360,6 +361,7 @@
             pltpu.VMEM((BLK, BLK), BF16),
             pltpu.VMEM((BLK, BLK), BF16),
             pltpu.VMEM((NS, CH, BLK), BF16),
+            pltpu.VMEM((NS, CH, HALF), BF16),
             pltpu.VMEM((NS, *quarters), BF16),
             pltpu.VMEM((NS, 2, *quarters), BF16),
             pltpu.VMEM((NS, 2, *quarters), BF16),
@@ -380,7 +382,7 @@
             pltpu.VMEM((8, 128), F32),
             pltpu.VMEM((3, 8, 128), F32),
             dma((2,)),
-            *both((2,)),
+            *both((3,)),
             *both((NS,)),
             *both((NS, 3)),
             *both((NS, 2, 2)),

time: 201 us -> 189 us (0.940)
  Pallas kernels: 198 us -> 186 us
    pallas_call x1, Pallas kernels: 198 us -> 186 us  [on_device(): pl.pallas_call(step_kernel, name='cayley_step', out_shape=(jax.ShapeDtype...]
where the time goes in v2:
time: 189 us
  Pallas kernels  186 us (98%)
  local copies, waits for them, and re-layouts  2.44 us (1%)
    pallas_call x1, Pallas kernels, on_device(): pl.pallas_call(step_kernel, name='cayley_step', out_shape=(jax.ShapeDtype...  186 us

profile of v2, /device:TPU:1, one launch (start us, length us, event | category | flops | bytes accessed | tf_op | source)
XLA Modules:
  0.0 188.8 jit_solution(1102254785894601473)
XLA Ops:
  0.6 185.7 %cayley_step.1 = (f32[512,256]{1,0:T(8,128)}, f32[2,128]{1,0:T(2,128)}) custom-call(bf16[512,1024]{1,0:T(8,128)(2,1)} %rot_hbm.1, bf16[512,1024]{1,0:T(8,128)(2,1)} %grad_hbm.1), custom_call_target="tpu_custom_call" | custom-call | flops 20000000000 | bytes 3000000 | tf_op jit(solution)/shard_map/cayley_step/pallas_call | solution.py:348
  186.4 0.0 copy-start
  186.4 1.9 copy.6
  188.2 0.0 copy-done
  188.2 0.6 copy.7
Async XLA Ops:
  186.4 1.9 copy-start

commit v3 on v2

--- a/solution.py
+++ b/solution.py
@@ -14,14 +14,16 @@
 HALF = 512
 TILE = 512
 ITEMS = 2 * NS
+CUT = 384
+WIDE = (BLK, CUT)
 
 
 def step_kernel(
     rot_hbm, grad_hbm, out_ref, norm_ref,
-    rot, grad, base, base_out, panel, part, full, mine, ring_a, ring_b, swapped,
+    rot, grad, base, base_out, panel, part, full, mine, ring_a, ring_b, swapped, far, far_in, far_y,
     term, term_in, kept, tail, tail_in, upd, turned, turned_in, sq, sq_y, sq_sum, sq_in,
     load_sem, pair_s, pair_r, v0_s, v0_r, v1_s, v1_r, a_s, a_r, b_s, b_r, z_s, z_r,
-    c_s, c_r, e_s, e_r, t_s, t_r, w_s, w_r, u_s, u_r, n_s, n_r, m_s, m_r,
+    c_s, c_r, e_s, e_r, fa_s, fa_r, fb_s, fb_r, fc_s, fc_r, fd_s, fd_r, t_s, t_r, w_s, w_r, u_s, u_r, n_s, n_r, m_s, m_r,
 ):
     row = lax.axis_index("row")
     col = lax.axis_index("col")
@@ -101,34 +103,79 @@
         k = i % NS
         return send(panel.at[k, x], panel.at[k, x], v1_s.at[k, d], v1_r.at[k, d], x_all[d])
 
+    def first(h):
+        return pl.ds(0, WIDE[h])
+
     def ra(i, h, d):
         k = i % NS
         return send(
-            part.at[k, h, across, d], ring_a.at[k, h, d], a_s.at[k, h, d], a_r.at[k, h, d], y_dev[d]
+            part.at[k, h, across, d, :, first(h)],
+            ring_a.at[k, h, d, :, first(h)],
+            a_s.at[k, h, d],
+            a_r.at[k, h, d],
+            y_dev[d],
         )
 
     def rb(i, h, d):
         k = i % NS
         return send(
-            part.at[k, h, y_q[d]], ring_b.at[k, h, d], b_s.at[k, h, d], b_r.at[k, h, d], y_dev[d]
+            part.at[k, h, y_q[d], :, :, first(h)],
+            ring_b.at[k, h, d, :, :, first(h)],
+            b_s.at[k, h, d],
+            b_r.at[k, h, d],
+            y_dev[d],
         )
 
     def zx(i, h):
         k = i % NS
-        return send(mine.at[k, h], swapped.at[k, h], z_s.at[k, h], z_r.at[k, h], z_dev)
+        return send(
+            mine.at[k, h, :, :, first(h)], swapped.at[k, h, :, :, first(h)], z_s.at[k, h], z_r.at[k, h], z_dev
+        )
 
     def ga(i, h, d):
         k = i % NS
         return send(
-            full.at[k, h, y], full.at[k, h, y], c_s.at[k, h, d], c_r.at[k, h, d], y_dev[d]
+            full.at[k, h, y, :, :, first(h)],
+            full.at[k, h, y, :, :, first(h)],
+            c_s.at[k, h, d],
+            c_r.at[k, h, d],
+            y_dev[d],
         )
 
     def gb(i, h, d):
         k = i % NS
         q = y_q[1 - d]
         return send(
-            full.at[k, h, q, d], full.at[k, h, q, d], e_s.at[k, h, d], e_r.at[k, h, d], y_dev[d]
-        )
+            full.at[k, h, q, d, :, first(h)],
+            full.at[k, h, q, d, :, first(h)],
+            e_s.at[k, h, d],
+            e_r.at[k, h, d],
+            y_dev[d],
+        )
+
+    rest = pl.ds(CUT, BLK - CUT)
+
+    def fa(i):
+        k = i % NS
+        return send(
+            part.at[k, 1, :, 1 - zh, :, rest], far_in.at[k], fa_s.at[k], fa_r.at[k], z_dev
+        )
+
+    def fb(i, d):
+        k = i % NS
+        return send(
+            far.at[k, (y + d + 1) % 4], far_y.at[k, d], fb_s.at[k, d], fb_r.at[k, d], y_all[d]
+        )
+
+    def fc(i, d):
+        k = i % NS
+        place = full.at[k, 1, y, zh, :, rest]
+        return send(place, place, fc_s.at[k, d], fc_r.at[k, d], y_all[d])
+
+    def fd(i):
+        k = i % NS
+        place = full.at[k, 1, :, zh, :, rest]
+        return send(place, place, fd_s.at[k], fd_r.at[k], z_dev)
 
     def tx(i, d):
         k = i % NS
@@ -182,6 +229,12 @@
         def stage(late):
             return pl.when((i >= late) & (i < ITEMS + late))
 
+        @pl.when((i > NS) & (i <= ITEMS))
+        def _():
+            v0(i - 1).wait_recv()
+            for d in range(3):
+                v1(i - 1, d).start()
+
         @stage(5)
         def _():
             it = i - 5
@@ -192,6 +245,8 @@
                     gb(it, h, d).start()
             for h in range(2):
                 zx(it, h).wait_send()
+            for d in range(3):
+                fc(it, d).wait_send()
 
         @stage(4)
         def _():
@@ -199,12 +254,15 @@
             k = it % NS
             for h in range(2):
                 zx(it, h).wait_recv()
-                z = mine[k, h].astype(F32) + swapped[k, h].astype(F32)
-                full[k, h, y] = z.astype(BF16)
+                w = first(h)
+                z = mine[k, h, :, :, w].astype(F32) + swapped[k, h, :, :, w].astype(F32)
+                full[k, h, y, :, :, w] = z.astype(BF16)
                 for d in range(2):
                     ga(it, h, d).start()
             for h, d in every:
                 rb(it, h, d).wait_send()
+            for d in range(3):
+                fb(it, d).wait_send()
 
         @stage(3)
         def _():
@@ -213,13 +271,23 @@
             for h in range(2):
                 for d in range(2):
                     rb(it, h, d).wait_recv()
-                s = part[k, h, y].astype(F32) + (
-                    ring_b[k, h, 0].astype(F32) + ring_b[k, h, 1].astype(F32)
+                w = first(h)
+                s = part[k, h, y, :, :, w].astype(F32) + (
+                    ring_b[k, h, 0, :, :, w].astype(F32) + ring_b[k, h, 1, :, :, w].astype(F32)
                 )
-                mine[k, h] = s.astype(BF16)
+                mine[k, h, :, :, w] = s.astype(BF16)
                 zx(it, h).start()
+            for d in range(3):
+                fb(it, d).wait_recv()
+            s = (far[k, y].astype(F32) + far_y[k, 0].astype(F32)) + (
+                far_y[k, 1].astype(F32) + far_y[k, 2].astype(F32)
+            )
+            full[k, 1, y, zh, :, rest] = s.astype(BF16)
+            for d in range(3):
+                fc(it, d).start()
             for h, d in every:
                 ra(it, h, d).wait_send()
+            fa(it).wait_send()
 
         @stage(8)
         def _():
@@ -243,15 +311,28 @@
                 tx(it, d).wait_send()
             wz(it).wait_send()
 
+        @stage(4)
+        def _():
+            it = i - 4
+            for d in range(3):
+                fc(it, d).wait_recv()
+            fd(it).start()
+
         @stage(2)
         def _():
             it = i - 2
             k = it % NS
             for h, d in every:
                 ra(it, h, d).wait_recv()
-                total = part[k, h, y_q[d], d].astype(F32) + ring_a[k, h, d].astype(F32)
-                part[k, h, y_q[d], d] = total.astype(BF16)
+                w = first(h)
+                total = part[k, h, y_q[d], d, :, w].astype(F32) + ring_a[k, h, d, :, w].astype(F32)
+                part[k, h, y_q[d], d, :, w] = total.astype(BF16)
                 rb(it, h, d).start()
+            fa(it).wait_recv()
+            sums = part[k, 1, :, zh, :, rest].astype(F32) + far_in[k].astype(F32)
+            far[k] = sums.astype(BF16)
+            for d in range(3):
+                fb(it, d).start()
             for d in range(3):
                 v1(it, d).wait_send()
 
@@ -260,17 +341,13 @@
             it = i - 6
             for h, d in every:
                 gb(it, h, d).wait_recv()
+            fd(it).wait_recv()
             apply(it)
             for d in range(3):
                 tx(it, d).start()
             for h, d in every:
                 ga(it, h, d).wait_send()
-
-        @pl.when((i >= NS) & (i < ITEMS))
-        def _():
-            v0(i).wait_recv()
-            for d in range(3):
-                v1(i, d).start()
+            fd(it).wait_send()
 
         @stage(7)
         def _():
@@ -296,9 +373,11 @@
             for d in range(3):
                 v1(it, d).wait_recv()
             for h in range(2):
-                project(it, h)
+                project(it, 1 - h)
+                if h == 0:
+                    fa(it).start()
                 for d in range(2):
-                    ra(it, h, d).start()
+                    ra(it, 1 - h, d).start()
             v0(it).wait_send()
 
         return 0
@@ -369,6 +448,9 @@
             pltpu.VMEM((NS, 2, 2, CH, BLK), BF16),
             pltpu.VMEM((NS, 2, 2, 2, CH, BLK), BF16),
             pltpu.VMEM((NS, 2, 2, CH, BLK), BF16),
+            pltpu.VMEM((NS, 4, CH, BLK - CUT), BF16),
+            pltpu.VMEM((NS, 4, CH, BLK - CUT), BF16),
+            pltpu.VMEM((NS, 3, CH, BLK - CUT), BF16),
             pltpu.VMEM((NS, *quarters), BF16),
             pltpu.VMEM((NS, 3, 2, CH, BLK), BF16),
             pltpu.VMEM((NS, CH, BLK), F32),
@@ -390,6 +472,10 @@
             *both((NS, 2)),
             *both((NS, 2, 2)),
             *both((NS, 2, 2)),
+            *both((NS,)),
+            *both((NS, 3)),
+            *both((NS, 3)),
+            *both((NS,)),
             *both((NS, 3)),
             *both((NS,)),
             *both((1,)),

time: 189 us -> 181 us (0.958)
  Pallas kernels: 186 us -> 178 us
    pallas_call x1, Pallas kernels: 186 us -> 178 us  [on_device(): pl.pallas_call(step_kernel, name='cayley_step', out_shape=(jax.ShapeDtype...]
where the time goes in v3:
time: 181 us
  Pallas kernels  178 us (98%)
  local copies, waits for them, and re-layouts  2.44 us (1%)
    pallas_call x1, Pallas kernels, on_device(): pl.pallas_call(step_kernel, name='cayley_step', out_shape=(jax.ShapeDtype...  178 us

profile of v3, /device:TPU:1, one launch (start us, length us, event | category | flops | bytes accessed | tf_op | source)
XLA Modules:
  0.0 180.8 jit_solution(12304779114566016223)
XLA Ops:
  0.6 177.7 %cayley_step.1 = (f32[512,256]{1,0:T(8,128)}, f32[2,128]{1,0:T(2,128)}) custom-call(bf16[512,1024]{1,0:T(8,128)(2,1)} %rot_hbm.1, bf16[512,1024]{1,0:T(8,128)(2,1)} %grad_hbm.1), custom_call_target="tpu_custom_call" | custom-call | flops 20000000000 | bytes 3000000 | tf_op jit(solution)/shard_map/cayley_step/pallas_call | solution.py:427
  178.4 0.0 copy-start
  178.4 1.9 %copy.6 = f32[512,256]{1,0:T(8,128)} copy(f32[512,256]{1,0:T(8,128)} %get-tuple-element.8) | data formatting | bytes 1048576
  180.2 0.0 copy-done
  180.2 0.6 copy.7
Async XLA Ops:
  178.4 1.9 %copy-start = (f32[2,128]{1,0:T(2,128)S(1)}, f32[2,128]{1,0:T(2,128)}, u32[]{:S(2)}) copy-start(f32[2,128]{1,0:T(2,128)} %get-tuple-element.5) | copy-start | bytes 3076

commit v4 on v3

v4 whole, which is shorter than its diff:
```python
import jax
import jax.numpy as jnp
from jax import lax
from jax.experimental import pallas as pl
from jax.experimental.pallas import tpu as pltpu
from jax.sharding import PartitionSpec as P

MESH = pl.DeviceIdType.MESH
F32 = jnp.float32
BF16 = jnp.bfloat16
NS = 8
CH = 16
BLK = 1024
HALF = 512
TILE = 512
ITEMS = 2 * NS
NQ = 2
NL = 4
CUT = 384
WIDE = (BLK, CUT)
EARLY = 0
LATE = ITEMS - 1


def step_kernel(
    rot_hbm, grad_hbm, out_ref, norm_ref,
    rot, grad, base, base_out, panel, part, full, mine, ring_a, ring_b, swapped, far, far_in, far_y,
    term, term_in, kept, tail, tail_in, upd, squares, turned, turned_in, sq, sq_y, sq_sum, sq_in,
    load_sem, pair_s, pair_r, v0_s, v0_r, v1_s, v1_r, a_s, a_r, b_s, b_r, z_s, z_r,
    c_s, c_r, e_s, e_r, fa_s, fa_r, fb_s, fb_r, fc_s, fc_r, fd_s, fd_r, t_s, t_r, w_s, w_r, u_s, u_r, n_s, n_r, m_s, m_r,
):
    row = lax.axis_index("row")
    col = lax.axis_index("col")
    core, y, zh = row % 2, (row // 2) % 4, row // 8
    x, zl = col // 2, col % 2
    up, across, down = (y + 1) % 4, (y + 2) % 4, (y + 3) % 4

    def at_row(zh_, y_, core_):
        return {"row": zh_ * 8 + y_ * 2 + core_, "col": col}

    def at_col(x_, zl_):
        return {"row": row, "col": x_ * 2 + zl_}

    pair = at_row(zh, y, 1 - core)
    y_dev = (at_row(zh, up, core), at_row(zh, down, core))
    y_q = (up, down)
    y_all = tuple(at_row(zh, (y + k) % 4, core) for k in (1, 2, 3))
    z_dev = at_row(1 - zh, y, core)
    zc_dev = at_row(1 - zh, y, 1 - core)
    x_all = tuple(at_col((x + k) % 4, zl) for k in (1, 2, 3))
    x_far = tuple(at_col((x + k) % 4, 1 - zl) for k in (1, 2, 3))
    zl_dev = at_col(x, 1 - zl)

    def send(src, dst, s, r, dev):
        return pltpu.make_async_remote_copy(
            src_ref=src, dst_ref=dst, send_sem=s, recv_sem=r, device_id=dev, device_id_type=MESH
        )

    own_rows = pl.ds(pl.multiple_of(core * HALF, HALF), HALF)
    other_rows = pl.ds(pl.multiple_of((1 - core) * HALF, HALF), HALF)
    loads = [
        pltpu.make_async_copy(rot_hbm, rot.at[own_rows], load_sem.at[0]),
        pltpu.make_async_copy(grad_hbm, grad.at[own_rows], load_sem.at[1]),
    ]
    for c in loads:
        c.start()

    barrier = pltpu.get_barrier_semaphore()
    peers = (pair, *y_all, z_dev, zc_dev, *x_all, *x_far, zl_dev)
    for dev in peers:
        pl.semaphore_signal(barrier, inc=1, device_id=dev, device_id_type=MESH)

    pick = lax.broadcasted_iota(jnp.int32, (128, HALF), 1) == 4 * lax.broadcasted_iota(
        jnp.int32, (128, HALF), 0
    )
    pick = pick.astype(F32).astype(BF16)

    def picked(side):
        cols = pl.ds(pl.multiple_of(side * HALF, HALF), HALF)
        return (
            lax.dot_general(
                pick, rot[own_rows, cols], (((1,), (1,)), ((), ())), preferred_element_type=F32
            )
            .astype(BF16)
            .reshape(NS, CH, HALF)
        )

    loads[0].wait()
    base_out[...] = picked(1 - core)
    base[:, :, own_rows] = picked(core)
    loads[1].wait()

    pl.semaphore_wait(barrier, len(peers))
    pairs = [
        send(base_out, base.at[:, :, own_rows], pair_s.at[0], pair_r.at[0], pair),
        send(rot.at[own_rows], rot.at[own_rows], pair_s.at[1], pair_r.at[1], pair),
        send(grad.at[own_rows], grad.at[own_rows], pair_s.at[2], pair_r.at[2], pair),
    ]
    for c in pairs:
        c.start()
    pairs[0].wait_recv()

    def first(h):
        return pl.ds(0, WIDE[h])

    rest = pl.ds(CUT, BLK - CUT)

    def v0(i):
        k = i % NS
        return send(panel.at[k, x, zl], panel.at[k, x, zl], v0_s.at[k], v0_r.at[k], zl_dev)

    def v1(i, d):
        k = i % NS
        return send(panel.at[k, x], panel.at[k, x], v1_s.at[k], v1_r.at[k], x_all[d])

    def v1_all(i):
        k = i % NS
        return send(term_in.at[k], term_in.at[k], v1_s.at[k], v1_r.at[k], zl_dev)

    def ra(i, h, d):
        k, q = i % NS, i % NQ
        return send(
            part.at[k, h, across, d, :, first(h)],
            ring_a.at[k, h, d, :, first(h)],
            a_s.at[q, h],
            a_r.at[q, h],
            y_dev[d],
        )

    def ra_all(i, h):
        k, q = i % NS, i % NQ
        ref = ring_a.at[k, h, :, :, first(h)]
        return send(ref, ref, a_s.at[q, h], a_r.at[q, h], zl_dev)

    def rb(i, h, d):
        k, q = i % NS, i % NQ
        return send(
            part.at[k, h, y_q[d], :, :, first(h)],
            ring_b.at[k, h, d, :, :, first(h)],
            b_s.at[q, h],
            b_r.at[q, h],
            y_dev[d],
        )

    def rb_all(i, h):
        k, q = i % NS, i % NQ
        ref = ring_b.at[k, h, :, :, :, first(h)]
        return send(ref, ref, b_s.at[q, h], b_r.at[q, h], zl_dev)

    def zx(i, h):
        k, q = i % NS, i % NQ
        return send(
            mine.at[k, h, :, :, first(h)],
            swapped.at[k, h, :, :, first(h)],
            z_s.at[q, h],
            z_r.at[q, h],
            z_dev,
        )

    def ga(i, h, d):
        k, q = i % NS, i % NL
        place = full.at[k, h, y, :, :, first(h)]
        return send(place, place, c_s.at[q, h], c_r.at[q, h], y_dev[d])

    def ga_all(i, h):
        k, q = i % NS, i % NL
        ref = ring_b.at[k, h, :, :, :, first(h)]
        return send(ref, ref, c_s.at[q, h], c_r.at[q, h], zl_dev)

    def gb(i, h, d):
        k, q = i % NS, i % NL
        place = full.at[k, h, y_q[1 - d], d, :, first(h)]
        return send(place, place, e_s.at[q, h], e_r.at[q, h], y_dev[d])

    def gb_all(i, h):
        k, q = i % NS, i % NL
        ref = ring_a.at[k, h, :, :, first(h)]
        return send(ref, ref, e_s.at[q, h], e_r.at[q, h], zl_dev)

    def fa(i):
        k, q = i % NS, i % NL
        return send(
            part.at[k, 1, :, 1 - zh, :, rest], far_in.at[k], fa_s.at[q], fa_r.at[q], z_dev
        )

    def fb(i, d):
        k, q = i % NS, i % NQ
        return send(
            far.at[k, (y + d + 1) % 4], far_y.at[k, d], fb_s.at[q], fb_r.at[q], y_all[d]
        )

    def fb_all(i):
        k, q = i % NS, i % NQ
        return send(far_y.at[k], far_y.at[k], fb_s.at[q], fb_r.at[q], zl_dev)

    def fc(i, d):
        k, q = i % NS, i % NQ
        place = full.at[k, 1, y, zh, :, rest]
        return send(place, place, fc_s.at[q], fc_r.at[q], y_all[d])

    def fc_all(i):
        k, q = i % NS, i % NQ
        return send(far_y.at[k], far_y.at[k], fc_s.at[q], fc_r.at[q], zl_dev)

    def fd(i):
        k, q = i % NS, i % NL
        place = full.at[k, 1, :, zh, :, rest]
        return send(place, place, fd_s.at[q], fd_r.at[q], z_dev)

    def tx(i, d):
        k, q = i % NS, i % NL
        return send(
            term.at[k, (x + d + 1) % 4], term_in.at[k, d], t_s.at[q], t_r.at[q], x_all[d]
        )

    def tx_all(i):
        k, q = i % NS, i % NL
        return send(term_in.at[k], term_in.at[k], t_s.at[q], t_r.at[q], zl_dev)

    def wz(i):
        k, q = i % NS, i % NL
        return send(tail.at[k], tail_in.at[k], w_s.at[q], w_r.at[q], zl_dev)

    for j in range(NS):
        panel[j, x, zl] = base[j]
    for j in range(EARLY):
        for d in range(3):
            place = panel.at[j, x, zl]
            for dev in (x_all[d], x_far[d]):
                send(place, place, v1_s.at[j], v1_r.at[j], dev).start()
    for j in range(NS):
        v0(j).start()
    for j in range(NS):
        v0(j).wait_recv()
        if j >= EARLY:
            for d in range(3):
                v1(j, d).start()
    pairs[1].wait_recv()
    pairs[2].wait_recv()

    def project(i, h):
        k = i % NS
        held = (rot, grad)[h]
        lhs = panel[k].reshape(8 * CH, BLK)

        @pl.loop(0, BLK // TILE)
        def _(n):
            cols = pl.ds(pl.multiple_of(n * TILE, TILE), TILE)
            z = jnp.dot(lhs, held[:, cols], preferred_element_type=F32)
            part[k, h, :, :, :, cols] = z.astype(BF16).reshape(4, 2, CH, TILE)

    def apply(i):
        k = i % NS

        @pl.loop(0, BLK // TILE)
        def _(n):
            rows = pl.ds(pl.multiple_of(n * TILE, TILE), TILE)
            nt = (((1,), (1,)), ((), ()))
            t = lax.dot_general(
                full[k, 0].reshape(8 * CH, BLK), grad[rows, :], nt, preferred_element_type=F32
            ) - lax.dot_general(
                full[k, 1].reshape(8 * CH, BLK), rot[rows, :], nt, preferred_element_type=F32
            )
            term[k, :, :, :, rows] = t.astype(BF16).reshape(4, 2, CH, TILE)

    def run(i, _):
        def stage(late):
            return pl.when((i >= late) & (i < ITEMS + late))

        @pl.when((i > NS) & (i <= ITEMS))
        def _():
            v0(i - 1).wait_recv()
            for d in range(3):
                v1(i - 1, d).start()

        @stage(5)
        def _():
            it = i - 5
            for h in range(2):
                ga_all(it, h).wait_recv()
                for d in range(2):
                    gb(it, h, d).start()
            for h in range(2):
                zx(it, h).wait_send()
            fc_all(it).wait_send()

        @stage(4)
        def _():
            it = i - 4
            k = it % NS
            for h in range(2):
                zx(it, h).wait_recv()
                w = first(h)
                z = mine[k, h, :, :, w].astype(F32) + swapped[k, h, :, :, w].astype(F32)
                full[k, h, y, :, :, w] = z.astype(BF16)
                for d in range(2):
                    ga(it, h, d).start()
            for h in range(2):
                rb_all(it, h).wait_send()

        @stage(3)
        def _():
            it = i - 3
            k = it % NS
            for h in range(2):
                rb_all(it, h).wait_recv()
                w = first(h)
                s = part[k, h, y, :, :, w].astype(F32) + (
                    ring_b[k, h, 0, :, :, w].astype(F32) + ring_b[k, h, 1, :, :, w].astype(F32)
                )
                mine[k, h, :, :, w] = s.astype(BF16)
                zx(it, h).start()
            for h in range(2):
                ra_all(it, h).wait_send()

        @stage(8)
        def _():
            it = i - 8
            k = it % NS
            wz(it).wait_recv()
            applied = kept[k] + tail_in[k].astype(F32)
            b = base[k].astype(F32)

            @pl.when(i < ITEMS)
            def _():
                first = b + 0.25 * applied
                panel[k, x, zl] = (b + first).astype(BF16)
                v0(i).start()

            @pl.when(i >= ITEMS)
            def _():
                new = b + 0.125 * applied
                upd[k] = new
                lanes = new[:, :128] * new[:, :128]
                for r in range(1, BLK // 128):
                    lane = new[:, r * 128 : (r + 1) * 128]
                    lanes = lanes + lane * lane
                squares[k] = lanes

            tx_all(it).wait_send()
            wz(it).wait_send()

        @stage(2)
        def _():
            it = i - 2
            k = it % NS
            for h in range(2):
                w = first(h)
                ra_all(it, h).wait_recv()
                for d in range(2):
                    there = part[k, h, y_q[d], d, :, w].astype(F32)
                    there = there + ring_a[k, h, d, :, w].astype(F32)
                    part[k, h, y_q[d], d, :, w] = there.astype(BF16)
                    rb(it, h, d).start()
            v1_all(it).wait_send()

        @stage(6)
        def _():
            it = i - 6
            for h in range(2):
                gb_all(it, h).wait_recv()
            fd(it).wait_recv()
            apply(it)
            k, q = it % NS, it % NL

            @pl.when(it < LATE)
            def _():
                for d in range(3):
                    tx(it, d).start()

            @pl.when(it >= LATE)
            def _():
                for d in range(3):
                    for z, dev in ((0, x_all[d]), (1, x_far[d])):
                        src = term.at[k, (x + d + 1) % 4, zl + z - 2 * zl * z]
                        send(src, term_in.at[k, d, z], t_s.at[q], t_r.at[q], dev).start()
                send(term.at[k, x, 1 - zl], tail_in.at[k], w_s.at[q], w_r.at[q], zl_dev).start()

            for h in range(2):
                ga_all(it, h).wait_send()
            fd(it).wait_send()

        @stage(7)
        def _():
            it = i - 7
            k = it % NS
            tx_all(it).wait_recv()

            def summed(z):
                return (term[k, x, z].astype(F32) + term_in[k, 0, z].astype(F32)) + (
                    term_in[k, 1, z].astype(F32) + term_in[k, 2, z].astype(F32)
                )

            @pl.when(it < LATE)
            def _():
                tail[k] = summed(1 - zl).astype(BF16)
                wz(it).start()
                kept[k] = summed(zl)

            @pl.when(it >= LATE)
            def _():
                total = term[k, x, zl].astype(F32)
                for d in range(3):
                    total = total + (term_in[k, d, 0].astype(F32) + term_in[k, d, 1].astype(F32))
                kept[k] = total

            for h in range(2):
                gb_all(it, h).wait_send()

        @stage(4)
        def _():
            it = i - 4
            fc_all(it).wait_recv()
            fd(it).start()
            fb_all(it).wait_send()

        @stage(3)
        def _():
            it = i - 3
            k = it % NS
            fb_all(it).wait_recv()
            s = (far[k, y].astype(F32) + far_y[k, 0].astype(F32)) + (
                far_y[k, 1].astype(F32) + far_y[k, 2].astype(F32)
            )
            full[k, 1, y, zh, :, rest] = s.astype(BF16)
            for d in range(3):
                fc(it, d).start()
            fa(it).wait_send()

        @stage(1)
        def _():
            it = i - 1
            v1_all(it).wait_recv()
            for h in range(2):
                project(it, 1 - h)
                if h == 0:
                    fa(it).start()
                for d in range(2):
                    ra(it, 1 - h, d).start()
            v0(it).wait_send()

        @stage(2)
        def _():
            it = i - 2
            k = it % NS
            fa(it).wait_recv()
            sums = part[k, 1, :, zh, :, rest].astype(F32) + far_in[k].astype(F32)
            far[k] = sums.astype(BF16)
            for d in range(3):
                fb(it, d).start()

        return 0

    lax.fori_loop(1, ITEMS + 8, run, 0)

    total = jnp.sum(squares[...].reshape(128, 128).T, axis=0, keepdims=True)
    sq[...] = jnp.broadcast_to(total, (8, 128))
    ys = [send(sq, sq_y.at[k], n_s.at[0], n_r.at[0], y_all[k]) for k in range(3)]
    for c in ys:
        c.start()

    def turn(side, r):
        cols = pl.ds(pl.multiple_of(side * HALF + r * 128, 128), 128)
        return upd[:, :, cols].reshape(128, 128).T

    for r in range(HALF // 128):
        turned[r * 128 : (r + 1) * 128, :] = turn(1 - core, r)
    swap = send(turned, turned_in, u_s.at[0], u_r.at[0], pair)
    swap.start()
    for r in range(HALF // 128):
        out_ref[r * 128 : (r + 1) * 128, pl.ds(pl.multiple_of(core * 128, 128), 128)] = turn(core, r)
    ys_all = send(sq_y, sq_y, n_s.at[0], n_r.at[0], zl_dev)
    ys_all.wait_recv()
    sq_sum[...] = (sq[...] + sq_y[0]) + (sq_y[1] + sq_y[2])
    ms = [
        send(sq_sum, sq_in.at[k], m_s.at[0], m_r.at[0], dev)
        for k, dev in enumerate((z_dev, pair, zc_dev))
    ]
    for c in ms:
        c.start()
    swap.wait_recv()
    out_ref[:, pl.ds(pl.multiple_of((1 - core) * 128, 128), 128)] = turned_in[...]
    ms_all = send(sq_in, sq_in, m_s.at[0], m_r.at[0], zl_dev)
    ms_all.wait_recv()
    own_norm = jnp.sqrt(sq_sum[0:1, :] + sq_in[0, 0:1, :])
    other_norm = jnp.sqrt(sq_in[1, 0:1, :] + sq_in[2, 0:1, :])
    norm_ref[0:1, :] = jnp.where(core == 0, own_norm, other_norm)
    norm_ref[1:2, :] = jnp.where(core == 0, other_norm, own_norm)
    for c in (*pairs, swap, ys_all, ms_all):
        c.wait_send()


def on_device(rotation, gradient):
    dma = pltpu.SemaphoreType.DMA

    def both(shape):
        return [dma(shape), dma(shape)]

    quarters = (4, 2, CH, BLK)
    updated, norms = pl.pallas_call(
        step_kernel,
        name="cayley_step",
        out_shape=(
            jax.ShapeDtypeStruct((HALF, 256), F32),
            jax.ShapeDtypeStruct((2, 128), F32),
        ),
        in_specs=[pl.BlockSpec(memory_space=pl.ANY)] * 2,
        out_specs=(
            pl.BlockSpec(memory_space=pltpu.VMEM),
            pl.BlockSpec(memory_space=pltpu.VMEM),
        ),
        scratch_shapes=[
            pltpu.VMEM((BLK, BLK), BF16),
            pltpu.VMEM((BLK, BLK), BF16),
            pltpu.VMEM((NS, CH, BLK), BF16),
            pltpu.VMEM((NS, CH, HALF), BF16),
            pltpu.VMEM((NS, *quarters), BF16),
            pltpu.VMEM((NS, 2, *quarters), BF16),
            pltpu.VMEM((NS, 2, *quarters), BF16),
            pltpu.VMEM((NS, 2, 2, CH, BLK), BF16),
            pltpu.VMEM((NS, 2, 2, CH, BLK), BF16),
            pltpu.VMEM((NS, 2, 2, 2, CH, BLK), BF16),
            pltpu.VMEM((NS, 2, 2, CH, BLK), BF16),
            pltpu.VMEM((NS, 4, CH, BLK - CUT), BF16),
            pltpu.VMEM((NS, 4, CH, BLK - CUT), BF16),
            pltpu.VMEM((NS, 3, CH, BLK - CUT), BF16),
            pltpu.VMEM((NS, *quarters), BF16),
            pltpu.VMEM((NS, 3, 2, CH, BLK), BF16),
            pltpu.VMEM((NS, CH, BLK), F32),
            pltpu.VMEM((NS, CH, BLK), BF16),
            pltpu.VMEM((NS, CH, BLK), BF16),
            pltpu.VMEM((NS, CH, BLK), F32),
            pltpu.VMEM((NS, CH, 128), F32),
            pltpu.VMEM((HALF, 128), F32),
            pltpu.VMEM((HALF, 128), F32),
            pltpu.VMEM((8, 128), F32),
            pltpu.VMEM((3, 8, 128), F32),
            pltpu.VMEM((8, 128), F32),
            pltpu.VMEM((3, 8, 128), F32),
            dma((2,)),
            *both((3,)),
            *both((NS,)),
            *both((NS,)),
            *both((NQ, 2)),
            *both((NQ, 2)),
            *both((NQ, 2)),
            *both((NL, 2)),
            *both((NL, 2)),
            *both((NL,)),
            *both((NQ,)),
            *both((NQ,)),
            *both((NL,)),
            *both((NL,)),
            *both((NL,)),
            *both((1,)),
            *both((1,)),
            *both((1,)),
        ],
        compiler_params=pltpu.CompilerParams(
            collective_id=1, has_side_effects=True, vmem_limit_bytes=62 * 1024 * 1024
        ),
        cost_estimate=pl.CostEstimate(
            flops=20_000_000_000, bytes_accessed=3_000_000, transcendentals=0
        ),
    )(rotation, gradient)
    return updated, norms.reshape(256)


def solution(mesh):
    placed = (P("row", "col"), P("row", "col"))
    return jax.shard_map(
        on_device,
        mesh=mesh,
        in_specs=placed,
        out_specs=(P("row", "col"), P("col")),
        check_vma=False,
    )
```

time: 181 us -> 173 us (0.956)
  Pallas kernels: 178 us -> 170 us
    pallas_call x1, Pallas kernels: 178 us -> 170 us  [on_device(): pl.pallas_call(step_kernel, name='cayley_step', out_shape=(jax.ShapeDtype...]
where the time goes in v4:
time: 173 us
  Pallas kernels  170 us (98%)
  local copies, waits for them, and re-layouts  2.44 us (1%)
    pallas_call x1, Pallas kernels, on_device(): pl.pallas_call(step_kernel, name='cayley_step', out_shape=(jax.ShapeDtype...  170 us

profile of v4, /device:TPU:1, one launch (start us, length us, event | category | flops | bytes accessed | tf_op | source)
XLA Modules:
  0.0 173.3 jit_solution(16612537956495942351)
XLA Ops:
  0.6 170.2 %cayley_step.1 = (f32[512,256]{1,0:T(8,128)}, f32[2,128]{1,0:T(2,128)}) custom-call(bf16[512,1024]{1,0:T(8,128)(2,1)} %rot_hbm.1, bf16[512,1024]{1,0:T(8,128)(2,1)} %grad_hbm.1), custom_call_target="tpu_custom_call" | custom-call | flops 20000000000 | bytes 3000000 | tf_op jit(solution)/shard_map/cayley_step/pallas_call | solution.py:500
  170.9 0.0 copy-start
  170.9 1.9 %copy.6 = f32[512,256]{1,0:T(8,128)} copy(f32[512,256]{1,0:T(8,128)} %get-tuple-element.8) | data formatting | bytes 1048576
  172.7 0.0 copy-done
  172.7 0.6 copy.7
Async XLA Ops:
  170.9 1.9 %copy-start = (f32[2,128]{1,0:T(2,128)S(1)}, f32[2,128]{1,0:T(2,128)}, u32[]{:S(2)}) copy-start(f32[2,128]{1,0:T(2,128)} %get-tuple-element.5) | copy-start | bytes 3076

commit v5 on v4

--- a/solution.py
+++ b/solution.py
@@ -18,16 +18,15 @@
 NL = 4
 CUT = 384
 WIDE = (BLK, CUT)
-EARLY = 0
 LATE = ITEMS - 1
 
 
 def step_kernel(
     rot_hbm, grad_hbm, out_ref, norm_ref,
     rot, grad, base, base_out, panel, part, full, mine, ring_a, ring_b, swapped, far, far_in, far_y,
-    term, term_in, kept, tail, tail_in, upd, squares, turned, turned_in, sq, sq_y, sq_sum, sq_in,
+    term, term_in, kept, tail, tail_in, upd, squares, turned, turned_in, sq, sq_in,
     load_sem, pair_s, pair_r, v0_s, v0_r, v1_s, v1_r, a_s, a_r, b_s, b_r, z_s, z_r,
-    c_s, c_r, e_s, e_r, fa_s, fa_r, fb_s, fb_r, fc_s, fc_r, fd_s, fd_r, t_s, t_r, w_s, w_r, u_s, u_r, n_s, n_r, m_s, m_r,
+    c_s, c_r, e_s, e_r, fa_s, fa_r, fb_s, fb_r, fc_s, fc_r, fd_s, fd_r, t_s, t_r, w_s, w_r, u_s, u_r, n_s, n_r,
 ):
     row = lax.axis_index("row")
     col = lax.axis_index("col")
@@ -46,7 +45,6 @@
     y_q = (up, down)
     y_all = tuple(at_row(zh, (y + k) % 4, core) for k in (1, 2, 3))
     z_dev = at_row(1 - zh, y, core)
-    zc_dev = at_row(1 - zh, y, 1 - core)
     x_all = tuple(at_col((x + k) % 4, zl) for k in (1, 2, 3))
     x_far = tuple(at_col((x + k) % 4, 1 - zl) for k in (1, 2, 3))
     zl_dev = at_col(x, 1 - zl)
@@ -66,7 +64,7 @@
         c.start()
 
     barrier = pltpu.get_barrier_semaphore()
-    peers = (pair, *y_all, z_dev, zc_dev, *x_all, *x_far, zl_dev)
+    peers = (pair, *y_dev, z_dev, *x_all, zl_dev)
     for dev in peers:
         pl.semaphore_signal(barrier, inc=1, device_id=dev, device_id_type=MESH)
 
@@ -223,18 +221,12 @@
 
     for j in range(NS):
         panel[j, x, zl] = base[j]
-    for j in range(EARLY):
-        for d in range(3):
-            place = panel.at[j, x, zl]
-            for dev in (x_all[d], x_far[d]):
-                send(place, place, v1_s.at[j], v1_r.at[j], dev).start()
     for j in range(NS):
         v0(j).start()
     for j in range(NS):
         v0(j).wait_recv()
-        if j >= EARLY:
-            for d in range(3):
-                v1(j, d).start()
+        for d in range(3):
+            v1(j, d).start()
     pairs[1].wait_recv()
     pairs[2].wait_recv()
 
@@ -455,9 +447,16 @@
 
     total = jnp.sum(squares[...].reshape(128, 128).T, axis=0, keepdims=True)
     sq[...] = jnp.broadcast_to(total, (8, 128))
-    ys = [send(sq, sq_y.at[k], n_s.at[0], n_r.at[0], y_all[k]) for k in range(3)]
-    for c in ys:
+    sums = []
+    for z in range(2):
+        for k in range(4):
+            for c in range(2):
+                if (z, k, c) != (0, 0, 0):
+                    dev = at_row((zh + z) % 2, (y + k) % 4, (core + c) % 2)
+                    sums.append(send(sq, sq_in.at[row], n_s.at[0], n_r.at[0], dev))
+    for c in sums:
         c.start()
+    sq_in[row] = sq[...]
 
     def turn(side, r):
         cols = pl.ds(pl.multiple_of(side * HALF + r * 128, 128), 128)
@@ -469,24 +468,17 @@
     swap.start()
     for r in range(HALF // 128):
         out_ref[r * 128 : (r + 1) * 128, pl.ds(pl.multiple_of(core * 128, 128), 128)] = turn(core, r)
-    ys_all = send(sq_y, sq_y, n_s.at[0], n_r.at[0], zl_dev)
-    ys_all.wait_recv()
-    sq_sum[...] = (sq[...] + sq_y[0]) + (sq_y[1] + sq_y[2])
-    ms = [
-        send(sq_sum, sq_in.at[k], m_s.at[0], m_r.at[0], dev)
-        for k, dev in enumerate((z_dev, pair, zc_dev))
-    ]
-    for c in ms:
-        c.start()
     swap.wait_recv()
     out_ref[:, pl.ds(pl.multiple_of((1 - core) * 128, 128), 128)] = turned_in[...]
-    ms_all = send(sq_in, sq_in, m_s.at[0], m_r.at[0], zl_dev)
-    ms_all.wait_recv()
-    own_norm = jnp.sqrt(sq_sum[0:1, :] + sq_in[0, 0:1, :])
-    other_norm = jnp.sqrt(sq_in[1, 0:1, :] + sq_in[2, 0:1, :])
-    norm_ref[0:1, :] = jnp.where(core == 0, own_norm, other_norm)
-    norm_ref[1:2, :] = jnp.where(core == 0, other_norm, own_norm)
-    for c in (*pairs, swap, ys_all, ms_all):
+    others = sq_in.at[pl.ds(0, 15)]
+    sums_all = send(others, others, n_s.at[0], n_r.at[0], zl_dev)
+    sums_all.wait_recv()
+    for c in range(2):
+        total = sq_in[c, 0:1, :]
+        for r in range(c + 2, 16, 2):
+            total = total + sq_in[r, 0:1, :]
+        norm_ref[c : c + 1, :] = jnp.sqrt(total)
+    for c in (*pairs, swap, sums_all):
         c.wait_send()
 
 
@@ -534,9 +526,7 @@
             pltpu.VMEM((HALF, 128), F32),
             pltpu.VMEM((HALF, 128), F32),
             pltpu.VMEM((8, 128), F32),
-            pltpu.VMEM((3, 8, 128), F32),
-            pltpu.VMEM((8, 128), F32),
-            pltpu.VMEM((3, 8, 128), F32),
+            pltpu.VMEM((16, 8, 128), F32),
             dma((2,)),
             *both((3,)),
             *both((NS,)),
@@ -554,10 +544,9 @@
             *both((NL,)),
             *both((1,)),
             *both((1,)),
-            *both((1,)),
         ],
         compiler_params=pltpu.CompilerParams(
-            collective_id=1, has_side_effects=True, vmem_limit_bytes=62 * 1024 * 1024
+            collective_id=1, has_side_effects=True, vmem_limit_bytes=53 * 1024 * 1024
         ),
         cost_estimate=pl.CostEstimate(
             flops=20_000_000_000, bytes_accessed=3_000_000, transcendentals=0

time: 173 us -> 168 us (0.971)
  Pallas kernels: 170 us -> 166 us
    pallas_call x1, Pallas kernels: 170 us -> 166 us  [on_device(): pl.pallas_call(step_kernel, name='cayley_step', out_shape=(jax.ShapeDtype...]
where the time goes in v5:
time: 168 us
  Pallas kernels  166 us (99%)
    pallas_call x1, Pallas kernels, on_device(): pl.pallas_call(step_kernel, name='cayley_step', out_shape=(jax.ShapeDtype...  166 us

profile of v5, /device:TPU:1, one launch (start us, length us, event | category | flops | bytes accessed | tf_op | source)
XLA Modules:
  0.0 168.4 jit_solution(496420576838843703)
XLA Ops:
  0.6 166.4 %cayley_step.1 = (f32[512,256]{1,0:T(8,128)S(1)}, f32[2,128]{1,0:T(2,128)S(1)}) custom-call(bf16[512,1024]{1,0:T(8,128)(2,1)} %rot_hbm.1, bf16[512,1024]{1,0:T(8,128)(2,1)} %grad_hbm.1), custom_call_target="tpu_custom_call" | custom-call | flops 20000000000 | bytes 3000000 | tf_op jit(solution)/shard_map/cayley_step/pallas_call | solution.py:492
  167.0 0.8 copy.6
  167.8 0.6 copy.7

commit v6 on v5

--- a/solution.py
+++ b/solution.py
@@ -12,11 +12,11 @@
 CH = 16
 BLK = 1024
 HALF = 512
-TILE = 512
+TILE = 1024
 ITEMS = 2 * NS
 NQ = 2
 NL = 4
-CUT = 384
+CUT = 256
 WIDE = (BLK, CUT)
 LATE = ITEMS - 1
 
@@ -48,6 +48,7 @@
     x_all = tuple(at_col((x + k) % 4, zl) for k in (1, 2, 3))
     x_far = tuple(at_col((x + k) % 4, 1 - zl) for k in (1, 2, 3))
     zl_dev = at_col(x, 1 - zl)
+    zl_pair = {"row": zh * 8 + y * 2 + 1 - core, "col": x * 2 + 1 - zl}
 
     def send(src, dst, s, r, dev):
         return pltpu.make_async_remote_copy(
@@ -64,7 +65,7 @@
         c.start()
 
     barrier = pltpu.get_barrier_semaphore()
-    peers = (pair, *y_dev, z_dev, *x_all, zl_dev)
+    peers = (pair, *y_dev, z_dev, *x_all, zl_dev, zl_pair)
     for dev in peers:
         pl.semaphore_signal(barrier, inc=1, device_id=dev, device_id_type=MESH)
 
@@ -86,6 +87,7 @@
     loads[0].wait()
     base_out[...] = picked(1 - core)
     base[:, :, own_rows] = picked(core)
+    panel[0, x, zl, :, own_rows] = base[0, :, own_rows]
     loads[1].wait()
 
     pl.semaphore_wait(barrier, len(peers))
@@ -94,7 +96,11 @@
         send(rot.at[own_rows], rot.at[own_rows], pair_s.at[1], pair_r.at[1], pair),
         send(grad.at[own_rows], grad.at[own_rows], pair_s.at[2], pair_r.at[2], pair),
     ]
-    for c in pairs:
+    pairs[0].start()
+    there = panel.at[0, x, zl, :, own_rows]
+    send(there, there, v0_s.at[0], v0_r.at[0], zl_dev).start()
+    send(base_out.at[0], there, v0_s.at[0], v0_r.at[0], zl_pair).start()
+    for c in pairs[1:]:
         c.start()
     pairs[0].wait_recv()
 
@@ -219,9 +225,10 @@
         k, q = i % NS, i % NL
         return send(tail.at[k], tail_in.at[k], w_s.at[q], w_r.at[q], zl_dev)
 
-    for j in range(NS):
+    panel[0, x, zl, :, other_rows] = base[0, :, other_rows]
+    for j in range(1, NS):
         panel[j, x, zl] = base[j]
-    for j in range(NS):
+    for j in range(1, NS):
         v0(j).start()
     for j in range(NS):
         v0(j).wait_recv()

time: 168 us -> 164 us (0.976)
  Pallas kernels: 166 us -> 162 us
    pallas_call x1, Pallas kernels: 166 us -> 162 us  [on_device(): pl.pallas_call(step_kernel, name='cayley_step', out_shape=(jax.ShapeDtype...]
where the time goes in v6:
time: 164 us
  Pallas kernels  162 us (99%)
    pallas_call x1, Pallas kernels, on_device(): pl.pallas_call(step_kernel, name='cayley_step', out_shape=(jax.ShapeDtype...  162 us

profile of v6, /device:TPU:1, one launch (start us, length us, event | category | flops | bytes accessed | tf_op | source)
XLA Modules:
  0.0 163.8 jit_solution(13970261530614626355)
XLA Ops:
  0.6 161.8 %cayley_step.1 = (f32[512,256]{1,0:T(8,128)S(1)}, f32[2,128]{1,0:T(2,128)S(1)}) custom-call(bf16[512,1024]{1,0:T(8,128)(2,1)} %rot_hbm.1, bf16[512,1024]{1,0:T(8,128)(2,1)} %grad_hbm.1), custom_call_target="tpu_custom_call" | custom-call | flops 20000000000 | bytes 3000000 | tf_op jit(solution)/shard_map/cayley_step/pallas_call | solution.py:499
  162.4 0.8 copy.6
  163.2 0.6 copy.7

commit v7 on v6

--- a/solution.py
+++ b/solution.py
@@ -122,7 +122,7 @@
         return send(term_in.at[k], term_in.at[k], v1_s.at[k], v1_r.at[k], zl_dev)
 
     def ra(i, h, d):
-        k, q = i % NS, i % NQ
+        k, q = i % NS, i % NL
         return send(
             part.at[k, h, across, d, :, first(h)],
             ring_a.at[k, h, d, :, first(h)],
@@ -132,7 +132,7 @@
         )
 
     def ra_all(i, h):
-        k, q = i % NS, i % NQ
+        k, q = i % NS, i % NL
         ref = ring_a.at[k, h, :, :, first(h)]
         return send(ref, ref, a_s.at[q, h], a_r.at[q, h], zl_dev)
 
@@ -226,11 +226,20 @@
         return send(tail.at[k], tail_in.at[k], w_s.at[q], w_r.at[q], zl_dev)
 
     panel[0, x, zl, :, other_rows] = base[0, :, other_rows]
+
+    def block_to_all(z):
+        place = panel.at[0, x, z]
+        for d in range(3):
+            send(place, place, v1_s.at[0], v1_r.at[0], x_all[d]).start()
+
+    block_to_all(zl)
     for j in range(1, NS):
         panel[j, x, zl] = base[j]
     for j in range(1, NS):
         v0(j).start()
-    for j in range(NS):
+    v0(0).wait_recv()
+    block_to_all(1 - zl)
+    for j in range(1, NS):
         v0(j).wait_recv()
         for d in range(3):
             v1(j, d).start()
@@ -426,9 +435,9 @@
                 fc(it, d).start()
             fa(it).wait_send()
 
-        @stage(1)
-        def _():
-            it = i - 1
+        @pl.when((i != NS) & (i <= ITEMS))
+        def _():
+            it = i - i // (NS + 1)
             v1_all(it).wait_recv()
             for h in range(2):
                 project(it, 1 - h)
@@ -450,7 +459,7 @@
 
         return 0
 
-    lax.fori_loop(1, ITEMS + 8, run, 0)
+    lax.fori_loop(0, ITEMS + 8, run, 0)
 
     total = jnp.sum(squares[...].reshape(128, 128).T, axis=0, keepdims=True)
     sq[...] = jnp.broadcast_to(total, (8, 128))
@@ -538,7 +547,7 @@
             *both((3,)),
             *both((NS,)),
             *both((NS,)),
-            *both((NQ, 2)),
+            *both((NL, 2)),
             *both((NQ, 2)),
             *both((NQ, 2)),
             *both((NL, 2)),

time: 164 us -> 162 us (0.988)
  Pallas kernels: 162 us -> 160 us
    pallas_call x1, Pallas kernels: 162 us -> 160 us  [on_device(): pl.pallas_call(step_kernel, name='cayley_step', out_shape=(jax.ShapeDtype...]
where the time goes in v7:
time: 162 us
  Pallas kernels  160 us (99%)
    pallas_call x1, Pallas kernels, on_device(): pl.pallas_call(step_kernel, name='cayley_step', out_shape=(jax.ShapeDtype...  160 us

profile of v7, /device:TPU:1, one launch (start us, length us, event | category | flops | bytes accessed | tf_op | source)
XLA Modules:
  0.0 161.7 jit_solution(12899876395773024231)
XLA Ops:
  0.6 159.7 %cayley_step.1 = (f32[512,256]{1,0:T(8,128)S(1)}, f32[2,128]{1,0:T(2,128)S(1)}) custom-call(bf16[512,1024]{1,0:T(8,128)(2,1)} %rot_hbm.1, bf16[512,1024]{1,0:T(8,128)(2,1)} %grad_hbm.1), custom_call_target="tpu_custom_call" | custom-call | flops 20000000000 | bytes 3000000 | tf_op jit(solution)/shard_map/cayley_step/pallas_call | solution.py:508
  160.3 0.8 copy.6
  161.1 0.6 copy.7

commit v8 on v7

--- a/solution.py
+++ b/solution.py
@@ -464,9 +464,9 @@
     total = jnp.sum(squares[...].reshape(128, 128).T, axis=0, keepdims=True)
     sq[...] = jnp.broadcast_to(total, (8, 128))
     sums = []
-    for z in range(2):
-        for k in range(4):
-            for c in range(2):
+    for z in (1, 0):
+        for k in (2, 1, 3, 0):
+            for c in (1, 0):
                 if (z, k, c) != (0, 0, 0):
                     dev = at_row((zh + z) % 2, (y + k) % 4, (core + c) % 2)
                     sums.append(send(sq, sq_in.at[row], n_s.at[0], n_r.at[0], dev))

time: 162 us -> 161 us (level)
  no operation moved by 1% of the time
where the time goes in v8:
time: 161 us
  Pallas kernels  159 us (99%)
    pallas_call x1, Pallas kernels, on_device(): pl.pallas_call(step_kernel, name='cayley_step', out_shape=(jax.ShapeDtype...  159 us

profile of v8, /device:TPU:1, one launch (start us, length us, event | category | flops | bytes accessed | tf_op | source)
XLA Modules:
  0.0 161.4 jit_solution(14087178126935445405)
XLA Ops:
  0.6 159.4 %cayley_step.1 = (f32[512,256]{1,0:T(8,128)S(1)}, f32[2,128]{1,0:T(2,128)S(1)}) custom-call(bf16[512,1024]{1,0:T(8,128)(2,1)} %rot_hbm.1, bf16[512,1024]{1,0:T(8,128)(2,1)} %grad_hbm.1), custom_call_target="tpu_custom_call" | custom-call | flops 20000000000 | bytes 3000000 | tf_op jit(solution)/shard_map/cayley_step/pallas_call | solution.py:508
  160.0 0.8 copy.6
  160.8 0.6 copy.7
